TPU v7x, 32 devices: a whole 2x2x4 slice. The times are simulated.
32 devices in a mesh: replica: 16 (over z, x, core), group: 2 (over y).
Axes of the slice: x: 2, y: 2, z: 4, core: 2. Of those that a mesh axis runs over, the one named last changes fastest.
Arguments:
- inputs: bfloat16 [640, 197, 384], P(('replica', 'group')), may hold values from -6 to 6
- cotangent: bfloat16 [640, 197, 384], P(('replica', 'group')), may hold values from -6 to 6
- gain_one: bfloat16 [384], P('group'), may hold values from 0.5 to 1.5
- shift_one: bfloat16 [384], P('group'), may hold values from -3 to 3
- w_qkv: bfloat16 [384, 1152], P('group'), may hold values from -2 to 2
- b_query: bfloat16 [384], P('group'), may hold values from -3 to 3
- b_value: bfloat16 [384], P('group'), may hold values from -3 to 3
- w_proj: bfloat16 [384, 384], P('group'), may hold values from -0.875 to 0.875
- b_proj: bfloat16 [384], P('group'), may hold values from -3 to 3
- gain_two: bfloat16 [384], P('group'), may hold values from 0.5 to 1.5
- shift_two: bfloat16 [384], P('group'), may hold values from -3 to 3
- w_fc1: bfloat16 [384, 1536], P('group'), may hold values from -0.3125 to 0.3125
- b_fc1: bfloat16 [1536], P('group'), may hold values from -3 to 3
- w_fc2: bfloat16 [1536, 384], P('group'), may hold values from -0.15625 to 0.15625
- b_fc2: bfloat16 [384], P('group'), may hold values from -3 to 3
Outputs:
- outputs: bfloat16 [640, 197, 384], P(('replica', 'group'))
- grad_inputs: float32 [640, 197, 384], P(('replica', 'group'))
- grad_gain_one: float32 [384], P('group')
- grad_shift_one: float32 [384], P('group')
- grad_w_qkv: float32 [384, 1152], P('group')
- grad_b_query: float32 [384], P('group')
- grad_b_value: float32 [384], P('group')
- grad_w_proj: float32 [384, 384], P('group')
- grad_b_proj: float32 [384], P('group')
- grad_gain_two: float32 [384], P('group')
- grad_shift_two: float32 [384], P('group')
- grad_w_fc1: float32 [384, 1536], P('group')
- grad_b_fc1: float32 [1536], P('group')
- grad_w_fc2: float32 [1536, 384], P('group')
- grad_b_fc2: float32 [384], P('group')
All inputs are finite; a program needn't handle non-finite values.
Results may differ from a plain program's by a relative error of at most 0.012.
Values may be sent and summed in bfloat16 or wider, within the bound.
A program may use at most 256 MiB of HBM per device.

v0:
```python
import jax
import jax.numpy as jnp
from jax import lax
from jax.sharding import PartitionSpec as P

HEADS = 6
epsilon = 1e-06


def product(left, right):
    return jnp.dot(left, right, preferred_element_type=jnp.float32)


def product_left_t(left, right):
    return lax.dot_general(
        left, right, (((0,), (0,)), ((), ())), preferred_element_type=jnp.float32
    )


def product_right_t(left, right):
    return lax.dot_general(
        left, right, (((1,), (1,)), ((), ())), preferred_element_type=jnp.float32
    )


def layer_norm(token_rows, gain_row, shift_row):
    centre = jnp.mean(token_rows, axis=-1, keepdims=True)
    centered = token_rows - centre
    inverse = lax.rsqrt(jnp.mean(centered * centered, axis=-1, keepdims=True) + epsilon)
    normed = centered * inverse
    hidden = (normed * gain_row.astype(jnp.float32) + shift_row.astype(jnp.float32)).astype(
        jnp.bfloat16
    )
    return (normed, inverse, hidden)


def norm_backward(grad_hidden, normed, inverse, gain_row):
    grad_normed = grad_hidden * gain_row.astype(jnp.float32)
    average_one = jnp.mean(grad_normed, axis=-1, keepdims=True)
    average_two = jnp.mean(grad_normed * normed, axis=-1, keepdims=True)
    grad_rows = inverse * (grad_normed - average_one - normed * average_two)
    return (grad_rows, jnp.sum(grad_hidden * normed, axis=0), jnp.sum(grad_hidden, axis=0))


def gelu_slope(values):
    return (
        0.5 * (1.0 + lax.erf(values * 0.7071067811865476))
        + values * jnp.exp(-0.5 * values * values) * 0.3989422804014327
    )


def attention_scores(query, keys, scaling):
    return jnp.einsum("bshe,bthe->bhst", query, keys, preferred_element_type=jnp.float32) * scaling


def forward_pass(inputs, params):
    (
        gain_one,
        shift_one,
        w_qkv,
        b_query,
        b_value,
        w_proj,
        b_proj,
        gain_two,
        shift_two,
        w_fc1,
        b_fc1,
        w_fc2,
        b_fc2,
    ) = params
    images, length, width = inputs.shape
    head_dim = width // HEADS
    scaling = head_dim ** (-0.5)
    row_count = images * length
    token_rows = inputs.reshape(row_count, width).astype(jnp.float32)
    normed_one, inverse_one, hidden_one = layer_norm(token_rows, gain_one, shift_one)
    bias_full = jnp.concatenate([b_query, jnp.zeros_like(b_query), b_value]).astype(jnp.float32)
    packed = (product(hidden_one, w_qkv) + bias_full).astype(jnp.bfloat16)
    packed = packed.reshape(images, length, 3, HEADS, head_dim)
    query = packed[:, :, 0]
    keys = packed[:, :, 1]
    values = packed[:, :, 2]
    scores = attention_scores(query, keys, scaling)
    log_total = jax.nn.logsumexp(scores, axis=-1, keepdims=True)
    probs_b = jnp.exp(scores - log_total).astype(jnp.bfloat16)
    attended = jnp.einsum("bhst,bthe->bshe", probs_b, values, preferred_element_type=jnp.float32)
    attended = attended.astype(jnp.bfloat16).reshape(row_count, width)
    resid = token_rows + product(attended, w_proj) + b_proj.astype(jnp.float32)
    normed_two, inverse_two, hidden_two = layer_norm(resid, gain_two, shift_two)
    pre_act = product(hidden_two, w_fc1) + b_fc1.astype(jnp.float32)
    act_b = jax.nn.gelu(pre_act, approximate=False).astype(jnp.bfloat16)
    outputs = (resid + product(act_b, w_fc2) + b_fc2.astype(jnp.float32)).astype(jnp.bfloat16)
    saved = (
        normed_one,
        inverse_one,
        hidden_one,
        query,
        keys,
        values,
        log_total,
        attended,
        normed_two,
        inverse_two,
        hidden_two,
        pre_act,
        act_b,
    )
    return (outputs.reshape(images, length, width), saved)


def backward_pass(cotangent, saved, params):
    (
        gain_one,
        shift_one,
        w_qkv,
        b_query,
        b_value,
        w_proj,
        b_proj,
        gain_two,
        shift_two,
        w_fc1,
        b_fc1,
        w_fc2,
        b_fc2,
    ) = params
    (
        normed_one,
        inverse_one,
        hidden_one,
        query,
        keys,
        values,
        log_total,
        attended,
        normed_two,
        inverse_two,
        hidden_two,
        pre_act,
        act_b,
    ) = saved
    images, length, width = cotangent.shape
    head_dim = width // HEADS
    scaling = head_dim ** (-0.5)
    row_count = images * length
    grad_out = cotangent.reshape(row_count, width)
    grad_top = grad_out.astype(jnp.float32)
    grad_b_fc2 = jnp.sum(grad_top, axis=0)
    grad_w_fc2 = product_left_t(act_b, grad_out)
    grad_pre = product_right_t(grad_out, w_fc2) * gelu_slope(pre_act)
    grad_b_fc1 = jnp.sum(grad_pre, axis=0)
    grad_pre_b = grad_pre.astype(jnp.bfloat16)
    grad_w_fc1 = product_left_t(hidden_two, grad_pre_b)
    grad_hidden_two = product_right_t(grad_pre_b, w_fc1)
    grad_part, grad_gain_two, grad_shift_two = norm_backward(
        grad_hidden_two, normed_two, inverse_two, gain_two
    )
    grad_resid = grad_top + grad_part
    grad_b_proj = jnp.sum(grad_resid, axis=0)
    grad_resid_b = grad_resid.astype(jnp.bfloat16)
    grad_w_proj = product_left_t(attended, grad_resid_b)
    grad_attended = product_right_t(grad_resid_b, w_proj).astype(jnp.bfloat16)
    grad_attended = grad_attended.reshape(images, length, HEADS, head_dim)
    probs = jnp.exp(attention_scores(query, keys, scaling) - log_total)
    probs_b = probs.astype(jnp.bfloat16)
    grad_values = jnp.einsum(
        "bhst,bshe->bthe", probs_b, grad_attended, preferred_element_type=jnp.float32
    )
    grad_probs = jnp.einsum(
        "bshe,bthe->bhst", grad_attended, values, preferred_element_type=jnp.float32
    )
    delta_rows = jnp.sum(probs * grad_probs, axis=-1, keepdims=True)
    grad_scores = (probs * (grad_probs - delta_rows) * scaling).astype(jnp.bfloat16)
    grad_query = jnp.einsum(
        "bhst,bthe->bshe", grad_scores, keys, preferred_element_type=jnp.float32
    )
    grad_keys = jnp.einsum(
        "bhst,bshe->bthe", grad_scores, query, preferred_element_type=jnp.float32
    )
    grad_b_query = jnp.sum(grad_query.reshape(row_count, width), axis=0)
    grad_b_value = jnp.sum(grad_values.reshape(row_count, width), axis=0)
    grad_packed_b = (
        jnp.stack([grad_query, grad_keys, grad_values], axis=2)
        .reshape(row_count, 3 * width)
        .astype(jnp.bfloat16)
    )
    grad_w_qkv = product_left_t(hidden_one, grad_packed_b)
    grad_hidden_one = product_right_t(grad_packed_b, w_qkv)
    grad_first, grad_gain_one, grad_shift_one = norm_backward(
        grad_hidden_one, normed_one, inverse_one, gain_one
    )
    grad_inputs = (grad_resid + grad_first).reshape(images, length, width)
    grads = (
        grad_gain_one,
        grad_shift_one,
        grad_w_qkv,
        grad_b_query,
        grad_b_value,
        grad_w_proj,
        grad_b_proj,
        grad_gain_two,
        grad_shift_two,
        grad_w_fc1,
        grad_b_fc1,
        grad_w_fc2,
        grad_b_fc2,
    )
    return (grad_inputs, grads)


def owned_rows(whole, position, members):
    share = whole.shape[0] // members
    return lax.dynamic_slice_in_dim(whole, position * share, share, 0)


def local(
    inputs,
    cotangent,
    gain_one,
    shift_one,
    w_qkv,
    b_query,
    b_value,
    w_proj,
    b_proj,
    gain_two,
    shift_two,
    w_fc1,
    b_fc1,
    w_fc2,
    b_fc2,
):
    gathered = (
        lax.all_gather(gain_one, "group", axis=0, tiled=True),
        lax.all_gather(shift_one, "group", axis=0, tiled=True),
        lax.all_gather(w_qkv, "group", axis=0, tiled=True),
        lax.all_gather(b_query, "group", axis=0, tiled=True),
        lax.all_gather(b_value, "group", axis=0, tiled=True),
        lax.all_gather(w_proj, "group", axis=0, tiled=True),
        lax.all_gather(b_proj, "group", axis=0, tiled=True),
        lax.all_gather(gain_two, "group", axis=0, tiled=True),
        lax.all_gather(shift_two, "group", axis=0, tiled=True),
        lax.all_gather(w_fc1, "group", axis=0, tiled=True),
        lax.all_gather(b_fc1, "group", axis=0, tiled=True),
        lax.all_gather(w_fc2, "group", axis=0, tiled=True),
        lax.all_gather(b_fc2, "group", axis=0, tiled=True),
    )
    outputs, saved = forward_pass(inputs, gathered)
    params_back = (
        lax.all_gather(gain_one, "group", axis=0, tiled=True),
        lax.all_gather(shift_one, "group", axis=0, tiled=True),
        lax.all_gather(w_qkv, "group", axis=0, tiled=True),
        lax.all_gather(b_query, "group", axis=0, tiled=True),
        lax.all_gather(b_value, "group", axis=0, tiled=True),
        lax.all_gather(w_proj, "group", axis=0, tiled=True),
        lax.all_gather(b_proj, "group", axis=0, tiled=True),
        lax.all_gather(gain_two, "group", axis=0, tiled=True),
        lax.all_gather(shift_two, "group", axis=0, tiled=True),
        lax.all_gather(w_fc1, "group", axis=0, tiled=True),
        lax.all_gather(b_fc1, "group", axis=0, tiled=True),
        lax.all_gather(w_fc2, "group", axis=0, tiled=True),
        lax.all_gather(b_fc2, "group", axis=0, tiled=True),
    )
    grad_inputs, grads = backward_pass(cotangent, saved, params_back)
    (
        term_gain_one,
        term_shift_one,
        term_w_qkv,
        term_b_query,
        term_b_value,
        term_w_proj,
        term_b_proj,
        term_gain_two,
        term_shift_two,
        term_w_fc1,
        term_b_fc1,
        term_w_fc2,
        term_b_fc2,
    ) = grads
    wholes = lax.psum(
        (
            term_gain_one,
            term_shift_one,
            term_w_qkv,
            term_b_query,
            term_b_value,
            term_w_proj,
            term_b_proj,
            term_gain_two,
            term_shift_two,
            term_w_fc1,
            term_b_fc1,
            term_w_fc2,
            term_b_fc2,
        ),
        ("replica", "group"),
    )
    position = lax.axis_index("group")
    members = lax.axis_size("group")
    totals = tuple((owned_rows(whole, position, members) for whole in wholes))
    token_total = (
        inputs.shape[0] * inputs.shape[1] * lax.axis_size("replica") * lax.axis_size("group")
    )
    factor = float(token_total) ** (-0.5)
    return (outputs, grad_inputs) + tuple((total * factor for total in totals))


def solution(mesh):
    return jax.shard_map(
        local,
        mesh=mesh,
        in_specs=(
            P(("replica", "group"), None, None),
            P(("replica", "group"), None, None),
            P("group"),
            P("group"),
            P("group", None),
            P("group"),
            P("group"),
            P("group", None),
            P("group"),
            P("group"),
            P("group"),
            P("group", None),
            P("group"),
            P("group", None),
            P("group"),
        ),
        out_specs=(
            P(("replica", "group"), None, None),
            P(("replica", "group"), None, None),
            P("group"),
            P("group"),
            P("group", None),
            P("group"),
            P("group"),
            P("group", None),
            P("group"),
            P("group"),
            P("group"),
            P("group", None),
            P("group"),
            P("group", None),
            P("group"),
        ),
        check_vma=False,
    )
```

profile of v0, /device:TPU:0, one launch (start us, length us, event | category | flops | bytes accessed | tf_op | source)
XLA Modules:
  0.0 717.0 jit_solution(14712015260770157017)
XLA Ops:
  41.6 6.7 all-reduce.10
  53.7 15.1 %all_gather.47 = bf16[384,1152]{1,0:T(8,128)(2,1)S(1)} all-gather(bf16[192,1152]{1,0:T(8,128)(2,1)S(1)} %copy-done.18), channel_id=1, replica_groups=mesh['replica'=16,'group'=2] {'group'}, dimensions={0}, use_global_device_ids=true | all-gather | bytes 1327104 | tf_op jit(solution)/shard_map/all_gather | solution.py:237
  72.2 8.7 %fusion.17 = bf16[3940,1152]{1,0:T(8,128)(2,1)} fusion(bf16[384,1152]{1,0:T(8,128)(2,1)S(1)} %all_gather.47, f32[1152]{0:T(1024)S(1)} %maximum_convert_fusion.1, f32[3940,384]{1,0:T(8,128)S(1)} %copy-done.1, f32[384]{0:T(512)S(1)} %copy-done.27, f32[384]{0:T(512)S(1)} %copy-done.25, f32[3940]{0:T(1024)S(1)} %copy-done.23, f32[3940]{0:T(1024)S(1)} %div.27), kind=kOutput, calls=%fused_computation.34 | convolution fusion | flops 3502502400 | bytes 16053536 | tf_op jit(solution)/shard_map/dot_general | solution.py:11
  80.9 27.6 %reshape.236 = bf16[20,197,3,6,64]{4,3,2,1,0:T(8,128)(2,1)} reshape(bf16[3940,1152]{1,0:T(8,128)(2,1)} %fusion.17) | data formatting | bytes 18155520 | tf_op jit(solution)/shard_map/reshape | solution.py:80
  108.5 16.3 %fusion.67 = (bf16[20,197,1,6,64]{4,3,2,1,0:T(8,128)(2,1)}, bf16[20,197,1,6,64]{4,3,2,1,0:T(8,128)(2,1)}, bf16[20,197,1,6,64]{4,3,2,1,0:T(8,128)(2,1)}) fusion(bf16[20,197,3,6,64]{4,3,2,1,0:T(8,128)(2,1)} %reshape.236), kind=kLoop, calls=%fused_computation.116 | loop fusion | bytes 18155520 | tf_op jit(solution)/shard_map/slice | solution.py:81
  124.8 9.7 %copy.74 = bf16[20,197,1,6,64]{1,4,3,0,2:T(8,128)(2,1)} copy(bf16[20,197,1,6,64]{4,3,2,1,0:T(8,128)(2,1)} %get-tuple-element.46) | data formatting | bytes 6051840
  134.5 9.7 %copy.75 = bf16[20,197,1,6,64]{1,4,3,0,2:T(8,128)(2,1)} copy(bf16[20,197,1,6,64]{4,3,2,1,0:T(8,128)(2,1)} %get-tuple-element.48) | data formatting | bytes 6051840
  144.2 14.9 %multiply_reduce_fusion.1 = (f32[20,6,197]{2,1,0:T(8,128)S(1)}, f32[20,6,197,197]{2,3,1,0:T(8,128)}) fusion(bf16[20,197,1,6,64]{1,4,3,0,2:T(8,128)(2,1)} %copy.75, bf16[20,197,1,6,64]{1,4,3,0,2:T(8,128)(2,1)} %copy.74), kind=kOutput, calls=%fused_computation.32 | convolution fusion | flops 605396736 | bytes 24774720 | tf_op jit(solution)/shard_map/bshe,bthe->bhst/dot_general | solution.py:53
  159.2 10.6 %exponential_reduce_fusion = f32[20,6,197]{2,1,0:T(8,128)S(1)} fusion(f32[20,6,197,197]{2,3,1,0:T(8,128)} %get-tuple-element.50, f32[20,6,197]{2,1,0:T(8,128)S(1)} %is-finite_select_fusion), kind=kLoop, calls=%fused_computation.7 | loop fusion | flops 13947600 | bytes 18817440 | tf_op jit(solution)/shard_map/reduce_sum | solution.py:85
  169.8 10.0 %copy.73 = bf16[20,197,1,6,64]{1,4,3,0,2:T(8,128)(2,1)} copy(bf16[20,197,1,6,64]{4,3,2,1,0:T(8,128)(2,1)} %get-tuple-element.47) | data formatting | bytes 6051840
  179.8 15.8 %convert_bitcast_fusion = bf16[20,197,6,64]{1,3,2,0:T(8,128)(2,1)} fusion(bf16[20,197,1,6,64]{1,4,3,0,2:T(8,128)(2,1)} %copy.73, f32[20,6,197]{2,1,0:T(8,128)S(1)} %log_add_fusion, f32[20,6,197,197]{2,3,1,0:T(8,128)} %get-tuple-element.50), kind=kOutput, calls=%fused_computation.73 | convolution fusion | flops 611590464 | bytes 24774720 | tf_op jit(solution)/shard_map/bhst,bthe->bshe/dot_general | solution.py:87
  195.6 6.8 copy.57
  202.4 6.6 reshape.187
  232.4 62.6 %fusion.4 = (bf16[3940,1536]{1,0:T(8,128)(2,1)}, f32[3940,1536]{1,0:T(8,128)}) fusion(f32[1536]{0:T(1024)S(1)} %reshape.219, bf16[384,1536]{1,0:T(8,128)(2,1)} %all-gather.4.cloned.1.call-done, f32[3940,384]{1,0:T(8,128)} %copy-done.2, f32[384]{0:T(512)S(1)} %convert_element_type.115, f32[384]{0:T(512)S(1)} %convert_element_type.114, ...), kind=kOutput, calls=%fused_computation.10 | convolution fusion | flops 5054799360 | bytes 43583264 | tf_op jit(solution)/shard_map/dot_general | solution.py:11
  295.1 20.8 %fusion.71 = (f32[1536]{0:T(1024)}, bf16[3940,1536]{1,0:T(8,128)(2,1)}) fusion(f32[3940,1536]{1,0:T(8,128)} %get-tuple-element.54, f32[1536]{0:T(1024)S(1)} %reshape.219, bf16[3940,384]{1,0:T(8,128)(2,1)S(1)} %copy-done.8, bf16[1536,384]{1,0:T(8,128)(2,1)} %all-gather.6.cloned.1.call-done), kind=kOutput, calls=%fused_computation.118 | convolution fusion | flops 4720433664 | bytes 40528896 | tf_op jit(solution)/shard_map/dot_general | solution.py:21
  315.8 11.3 %fusion.27 = f32[384,1536]{1,0:T(8,128)} fusion(bf16[3940,1536]{1,0:T(8,128)(2,1)} %get-tuple-element.62, f32[3940,384]{1,0:T(8,128)S(1)} %copy-done.3, f32[384]{0:T(512)S(1)} %convert_element_type.115, f32[384]{0:T(512)S(1)} %convert_element_type.114, f32[3940]{0:T(1024)S(1)} %add_rsqrt_fusion.1, f32[3940]{0:T(1024)S(1)} %broadcast_multiply_fusion.5), kind=kOutput, calls=%fused_computation.49 | convolution fusion | flops 4655377920 | bytes 20549408 | tf_op jit(solution)/shard_map/dot_general | solution.py:15
  327.2 10.6 %multiply_reduce_fusion.3 = (f32[384]{0:T(512)S(1)}, f32[3940]{0:T(1024)S(1)}, f32[3940]{0:T(1024)S(1)}, f32[384]{0:T(512)S(1)}, f32[3940,384]{1,0:T(8,128)S(1)}) fusion(f32[3940,384]{1,0:T(8,128)S(1)} %copy-done.3, f32[3940]{0:T(1024)S(1)} %add_rsqrt_fusion.1, f32[3940]{0:T(1024)S(1)} %broadcast_multiply_fusion.5, f32[384]{0:T(512)S(1)} %convert_element_type.114, ...), kind=kOutput, calls=%fused_computation.43 | convolution fusion | flops 4661420544 | bytes 25454656 | tf_op jit(solution)/shard_map/dot_general | solution.py:21
  346.6 7.4 %reshape.237 = bf16[20,197,6,64]{3,2,1,0:T(8,128)(2,1)} reshape(bf16[3940,384]{1,0:T(8,128)(2,1)S(1)} %convolution_convert_fusion) | data formatting | bytes 6051840 | tf_op jit(solution)/shard_map/reshape | solution.py:164
  354.0 9.9 %copy.59 = bf16[20,197,6,64]{1,3,2,0:T(8,128)(2,1)} copy(bf16[20,197,6,64]{3,2,1,0:T(8,128)(2,1)} %reshape.237) | data formatting | bytes 6051840 | tf_op jit(solution)/shard_map/reshape | solution.py:164
  363.9 14.9 %fusion.36 = f32[20,6,197,197]{2,3,1,0:T(8,128)} fusion(bf16[20,197,6,64]{1,3,2,0:T(8,128)(2,1)} %copy.59, bf16[20,197,1,6,64]{1,4,3,0,2:T(8,128)(2,1)} %copy.73), kind=kOutput, calls=%fused_computation.69 | convolution fusion | flops 596106240 | bytes 24680160 | tf_op jit(solution)/shard_map/bshe,bthe->bhst/dot_general | solution.py:170
  378.9 36.2 %bitcast_reduce_fusion.1 = (f32[6,64]{1,0:T(8,128)S(1)}, bf16[20,6,64,197]{3,2,1,0:T(8,128)(2,1)}) fusion(f32[20,6,197,197]{2,3,1,0:T(8,128)} %fusion.36, f32[20,6,197]{2,1,0:T(8,128)S(1)} %copy-done.15, f32[20,6,197,197]{2,3,1,0:T(8,128)} %get-tuple-element.50, bf16[20,197,1,6,64]{1,4,3,0,2:T(8,128)(2,1)} %copy.75), kind=kOutput, calls=%fused_computation.39 | convolution fusion | flops 641069312 | bytes 43404576 | tf_op jit(solution)/shard_map/bhst,bthe->bshe/dot_general | solution.py:175
  415.1 41.0 %fusion.40 = bf16[20,197,1,6,64]{1,4,3,0,2:T(8,128)(2,1)} fusion(f32[20,6,197,197]{2,3,1,0:T(8,128)} %fusion.36, f32[20,6,197]{2,1,0:T(8,128)S(1)} %copy-done.15, f32[20,6,197,197]{2,3,1,0:T(8,128)} %get-tuple-element.50, bf16[20,197,1,6,64]{1,4,3,0,2:T(8,128)(2,1)} %copy.74), kind=kOutput, calls=%fused_computation.74 | convolution fusion | flops 638043776 | bytes 43403040 | tf_op jit(solution)/shard_map/bhst,bshe->bthe/dot_general | solution.py:178
  456.1 13.8 %bitcast_reduce_fusion = (f32[6,64]{1,0:T(8,128)S(1)}, bf16[20,6,64,197]{3,2,1,0:T(8,128)(2,1)}) fusion(bf16[20,197,6,64]{1,3,2,0:T(8,128)(2,1)} %copy.59, f32[20,6,197]{2,1,0:T(8,128)S(1)} %copy-done.15, f32[20,6,197,197]{2,3,1,0:T(8,128)} %get-tuple-element.50), kind=kOutput, calls=%fused_computation.38 | convolution fusion | flops 613103040 | bytes 24776256 | tf_op jit(solution)/shard_map/bhst,bshe->bthe/dot_general | solution.py:167
  469.9 7.1 maximum_convert_fusion
  477.1 9.9 %copy.64 = bf16[20,197,3,6,64]{1,0,4,3,2:T(8,128)(2,1)} copy(bf16[20,197,3,6,64]{1,4,3,0,2:T(8,128)(2,1)S(1)} %maximum_convert_fusion) | data formatting | bytes 18155520 | tf_op jit(solution)/shard_map/convert_element_type | solution.py:186
  486.9 20.8 %convert_element_type.127 = bf16[3940,1152]{0,1:T(8,128)(2,1)} reshape(bf16[20,197,3,6,64]{1,0,4,3,2:T(8,128)(2,1)} %copy.64) | data formatting | bytes 18155520 | tf_op jit(solution)/shard_map/convert_element_type | solution.py:186
  507.8 13.7 %multiply_reduce_fusion.4 = (f32[384]{0:T(512)S(1)}, f32[3940]{0:T(1024)S(1)}, f32[3940]{0:T(1024)S(1)}, f32[384]{0:T(512)S(1)}, f32[3940,384]{1,0:T(8,128)}) fusion(f32[3940,384]{1,0:T(8,128)} %reshape.192, f32[3940]{0:T(1024)S(1)} %copy-done.24, f32[3940]{0:T(1024)S(1)} %copy-done.22, f32[384]{0:T(512)S(1)} %copy-done.26, ...), kind=kOutput, calls=%fused_computation.44 | convolution fusion | flops 3499467776 | bytes 22133824 | tf_op jit(solution)/shard_map/dot_general | solution.py:21
  527.1 10.8 %fusion.73 = f32[1536,384]{1,0:T(8,128)} fusion(bf16[3940,1536]{1,0:T(8,128)(2,1)} %get-tuple-element.53, bf16[3940,384]{1,0:T(8,128)(2,1)S(1)} %copy-done.9), kind=kOutput, calls=%fused_computation.120 | convolution fusion | flops 4647813120 | bytes 17488896 | tf_op jit(solution)/shard_map/dot_general | solution.py:15
  537.9 11.0 %multiply_add_fusion = f32[3940,384]{1,0:T(8,128)} fusion(f32[3940,384]{1,0:T(8,128)} %copy-done, f32[3940,384]{1,0:T(8,128)} %get-tuple-element.56, f32[3940,384]{1,0:T(8,128)} %reshape.192, f32[3940]{0:T(1024)S(1)} %broadcast_multiply_fusion.1, f32[3940]{0:T(1024)S(1)} %broadcast_multiply_fusion.2, f32[384]{0:T(512)S(1)} %copy-done.26, ...), kind=kLoop, calls=%fused_computation.45 | loop fusion | flops 12103680 | bytes 24271936 | tf_op jit(solution)/shard_map/add | solution.py:193
  554.6 10.8 %add_convert_fusion.1 = bf16[3940,384]{1,0:T(8,128)(2,1)S(1)} fusion(f32[3940,384]{1,0:T(8,128)} %copy-done.2, bf16[3940,1536]{1,0:T(8,128)(2,1)} %get-tuple-element.53, bf16[1536,384]{1,0:T(8,128)(2,1)} %all-gather.6.cloned.1.call-done, f32[384]{0:T(512)S(1)} %copy-done.30), kind=kOutput, calls=%fused_computation.53 | convolution fusion | flops 4652352000 | bytes 22362624 | tf_op jit(solution)/shard_map/dot_general | solution.py:11
  567.9 39.7 %all-reduce.8 = (f32[384]{0:T(512)S(1)}, f32[384]{0:T(512)S(1)}, f32[384]{0:T(512)S(1)}, f32[384]{0:T(512)S(1)}, f32[384]{0:T(512)S(1)}, /*index=5*/f32[384]{0:T...) all-reduce(f32[384]{0:T(512)S(1)} %get-tuple-element.17, ...), channel_id=1, replica_groups=mesh['replica'=16,'group'=2] {'replica','group'}, use_global_device_ids=true, to_apply=%region_12.0 | all-reduce | flops 4608 | bytes 36864 | tf_op jit(solution)/shard_map/psum | solution.py:281
  613.3 89.2 %all-reduce.13.cloned.1.call-done = (f32[384,1152]{1,0:T(8,128)}, f32[384,384]{1,0:T(8,128)}, f32[384,1536]{1,0:T(8,128)}, f32[1536,384]{1,0:T(8,128)}) async-done(((f32[384,1152]{1,0:T(8,128)}, f32[384,384]{1,0:T(8,128)}, f32[384,1536]{1,0:T(8,128)}, f32[1536,384]{1,0:T(8,128)}), (f32[384,1152]{1,0:T(8,128)}, f32[384,384]{1,0:T(8,128)}, f32[384,1536]{1,0:T(8,128)}, ...) | async-done | bytes 7077904 | tf_op jit(solution)/shard_map/psum | solution.py:281
  (157 shorter events, 101.8 us)
Async XLA Ops:
  7.2 225.3 %all-gather.4.cloned.1.call-start = ((), (), s32[]{:S(2)}) async-start(), calls=%async_computation | async-start | bytes 1769472 | tf_op jit(solution)/shard_map/all_gather | solution.py:244
  7.9 287.1 %all-gather.6.cloned.1.call-start = ((), (), s32[]{:S(2)}) async-start(), calls=%async_computation.1 | async-start | bytes 1769472 | tf_op jit(solution)/shard_map/all_gather | solution.py:246
  8.7 693.8 %all-reduce.13.cloned.1.call-start = ((), (), s32[]{:S(2)}) async-start(), calls=%async_computation.2 | async-start | bytes 14155776 | tf_op jit(solution)/shard_map/psum | solution.py:281
  13.7 58.4 %copy-start.21 = (f32[3940]{0:T(1024)}, f32[3940]{0:T(1024)S(1)}, u32[]{:S(2)}) copy-start(f32[3940]{0:T(1024)S(1)} %div.27) | copy-start | bytes 47284
  17.1 36.6 %copy-start.18 = (bf16[192,1152]{1,0:T(8,128)(2,1)S(1)}, bf16[192,1152]{1,0:T(8,128)(2,1)}, u32[]{:S(2)}) copy-start(bf16[192,1152]{1,0:T(8,128)(2,1)} %param.19) | copy-start | bytes 1327108
  53.7 18.4 %copy-start.36 = (bf16[384]{0:T(512)(128)(2,1)S(1)}, bf16[384]{0:T(512)(128)(2,1)}, u32[]{:S(2)}) copy-start(bf16[384]{0:T(512)(128)(2,1)} %get-tuple-element.36) | copy-start | bytes 2308
  53.7 18.4 %copy-start.37 = (bf16[384]{0:T(512)(128)(2,1)S(1)}, bf16[384]{0:T(512)(128)(2,1)}, u32[]{:S(2)}) copy-start(bf16[384]{0:T(512)(128)(2,1)} %get-tuple-element.37) | copy-start | bytes 2308
  53.7 18.5 %copy-start.1 = (f32[3940,384]{1,0:T(8,128)S(1)}, f32[3940,384]{1,0:T(8,128)}, u32[]{:S(2)}) copy-start(f32[3940,384]{1,0:T(8,128)} %reshape.192) | copy-start | bytes 18155524
  53.7 18.5 %copy-start.23 = (f32[3940]{0:T(1024)S(1)}, f32[3940]{0:T(1024)}, u32[]{:S(2)}) copy-start(f32[3940]{0:T(1024)} %rsqrt.21) | copy-start | bytes 47284
  53.7 18.5 %copy-start.25 = (f32[384]{0:T(512)S(1)}, f32[384]{0:T(512)}, u32[]{:S(2)}) copy-start(f32[384]{0:T(512)} %convert_element_type.105) | copy-start | bytes 4612
  53.7 18.5 %copy-start.27 = (f32[384]{0:T(512)S(1)}, f32[384]{0:T(512)}, u32[]{:S(2)}) copy-start(f32[384]{0:T(512)} %convert_element_type.106) | copy-start | bytes 4612
  169.8 25.8 %copy-start.14 = (f32[20,6,197]{2,1,0:T(8,128)}, f32[20,6,197]{2,1,0:T(8,128)S(1)}, u32[]{:S(2)}) copy-start(f32[20,6,197]{2,1,0:T(8,128)S(1)} %log_add_fusion) | copy-start | bytes 283684
  195.6 13.4 %copy-start.35 = (bf16[384]{0:T(512)(128)(2,1)S(1)}, bf16[384]{0:T(512)(128)(2,1)}, u32[]{:S(2)}) copy-start(bf16[384]{0:T(512)(128)(2,1)} %get-tuple-element.40) | copy-start | bytes 2308
  195.6 13.4 %copy-start.19 = (bf16[192,384]{1,0:T(8,128)(2,1)S(1)}, bf16[192,384]{1,0:T(8,128)(2,1)}, u32[]{:S(2)}) copy-start(bf16[192,384]{1,0:T(8,128)(2,1)} %param.22) | copy-start | bytes 442372
  209.0 11.4 %copy-start.5 = (bf16[3940,384]{0,1:T(8,128)(2,1)}, bf16[3940,384]{0,1:T(8,128)(2,1)S(1)}, u32[]{:S(2)}) copy-start(bf16[3940,384]{0,1:T(8,128)(2,1)S(1)} %reshape.187) | copy-start | bytes 9077764
  220.5 8.9 %copy-start.7 = (bf16[20,197,384]{2,1,0:T(8,128)(2,1)S(1)}, bf16[20,197,384]{2,1,0:T(8,128)(2,1)}, u32[]{:S(2)}) copy-start(bf16[20,197,384]{2,1,0:T(8,128)(2,1)} %add_convert_fusion) | copy-start | bytes 9077764
  223.5 8.3 %copy-start.32 = (bf16[384]{0:T(512)(128)(2,1)S(1)}, bf16[384]{0:T(512)(128)(2,1)}, u32[]{:S(2)}) copy-start(bf16[384]{0:T(512)(128)(2,1)} %get-tuple-element.43) | copy-start | bytes 2308
  232.4 62.6 %copy-start.8 = (bf16[3940,384]{1,0:T(8,128)(2,1)S(1)}, bf16[3940,384]{1,0:T(8,128)(2,1)}, u32[]{:S(2)}) copy-start(bf16[3940,384]{1,0:T(8,128)(2,1)} %reshape.189) | copy-start | bytes 9077764
  295.1 20.8 %copy-start.3 = (f32[3940,384]{1,0:T(8,128)S(1)}, f32[3940,384]{1,0:T(8,128)}, u32[]{:S(2)}) copy-start(f32[3940,384]{1,0:T(8,128)} %copy-done.2) | copy-start | bytes 18155524
  315.8 11.3 %copy-start.38 = (bf16[384,1536]{1,0:T(8,128)(2,1)S(1)}, bf16[384,1536]{1,0:T(8,128)(2,1)}, u32[]{:S(2)}) copy-start(bf16[384,1536]{1,0:T(8,128)(2,1)} %all-gather.4.cloned.1.call-done) | copy-start | bytes 3538948
  363.9 14.9 %copy-start.15 = (f32[20,6,197]{2,1,0:T(8,128)S(1)}, f32[20,6,197]{2,1,0:T(8,128)}, u32[]{:S(2)}) copy-start(f32[20,6,197]{2,1,0:T(8,128)} %copy-done.14) | copy-start | bytes 283684
  486.9 20.8 %copy-start.17 = (bf16[384,1152]{1,0:T(8,128)(2,1)S(1)}, bf16[384,1152]{1,0:T(8,128)(2,1)}, u32[]{:S(2)}) copy-start(bf16[384,1152]{1,0:T(8,128)(2,1)} %copy-done.16) | copy-start | bytes 2654212
  486.9 20.8 %copy-start.22 = (f32[3940]{0:T(1024)S(1)}, f32[3940]{0:T(1024)}, u32[]{:S(2)}) copy-start(f32[3940]{0:T(1024)} %copy-done.21) | copy-start | bytes 47284
  486.9 20.8 %copy-start.24 = (f32[3940]{0:T(1024)S(1)}, f32[3940]{0:T(1024)}, u32[]{:S(2)}) copy-start(f32[3940]{0:T(1024)} %rsqrt.21) | copy-start | bytes 47284
  486.9 20.8 %copy-start.26 = (f32[384]{0:T(512)S(1)}, f32[384]{0:T(512)}, u32[]{:S(2)}) copy-start(f32[384]{0:T(512)} %convert_element_type.105) | copy-start | bytes 4612
  507.8 13.7 %copy-start.10 = (bf16[3940,1152]{0,1:T(8,128)(2,1)S(1)}, bf16[3940,1152]{0,1:T(8,128)(2,1)}, u32[]{:S(2)}) copy-start(bf16[3940,1152]{0,1:T(8,128)(2,1)} %convert_element_type.127) | copy-start | bytes 27233284
  507.8 13.7 %copy-start.11 = (bf16[3940,384]{1,0:T(8,128)(2,1)S(1)}, bf16[3940,384]{1,0:T(8,128)(2,1)}, u32[]{:S(2)}) copy-start(bf16[3940,384]{1,0:T(8,128)(2,1)} %convert_element_type.129) | copy-start | bytes 9077764
  521.5 5.6 copy-start.9
  548.9 5.8 copy-start.30
  554.6 13.2 %copy-start.28 = (f32[1536]{0:T(1024)S(1)}, f32[1536]{0:T(1024)}, u32[]{:S(2)}) copy-start(f32[1536]{0:T(1024)} %get-tuple-element.61) | copy-start | bytes 18436
  554.6 13.2 %copy-start.29 = (f32[384]{0:T(512)S(1)}, f32[384]{0:T(512)}, u32[]{:S(2)}) copy-start(f32[384]{0:T(512)} %convert_reduce_fusion) | copy-start | bytes 4612
  702.5 7.0 copy-start.20
  (10 other events, 38.6 us)
Sparse Core Ops, SparseCore 0:
  9.5 25.4 all-gather.3
  36.6 24.9 all-gather.5
  538.0 164.4 all-reduce.12
where the time goes:
time: 724 us; the launch traced here: 717 us
  matrix products  302 us (42%)
  local copies, waits for them, and re-layouts  174 us (24%)
  waiting for transfers between devices  90.6 us (13%)
  blocking collectives  71.9 us (10%)
  other arithmetic  62.9 us (9%)
  between operations  15.1 us (2%)
    psum x1, waiting for transfers between devices, local(): lax.psum((term_gain_one, term_shift_one, term_w_qkv, term_b_query, term_b...  89.2 us
    dot_general x4, matrix products, product(): return jnp.dot(left, right, preferred_element_type=jnp.float32)  87.4 us
    unnamed x100, local copies, waits for them, and re-layouts  49 us
    dot_general x4, matrix products, product_right_t(): lax.dot_general(left, right, (((1,), (1,)), ((), ())), preferred_element_...  47.4 us
    dot_general x1, matrix products, backward_pass(): jnp.einsum('bhst,bshe->bthe', grad_scores, query, preferred_element_type=...  41 us
    psum x1, blocking collectives, local(): lax.psum((term_gain_one, term_shift_one, term_w_qkv, term_b_query, term_b...  39.7 us
    dot_general x1, matrix products, backward_pass(): jnp.einsum('bhst,bthe->bshe', grad_scores, keys, preferred_element_type=j...  36.2 us
    convert_element_type x2, local copies, waits for them, and re-layouts, backward_pass(): grad_packed_b = jnp.stack([grad_query, grad_keys, grad_values], axis=2).r...  30.7 us
  transfers between devices with their start and end apart: 3, of which 1 were waited for; matrix products, arithmetic and copies ran while one was open for 40% of the time, Pallas kernels for 0%

commit v1 on v0

--- a/solution.py
+++ b/solution.py
@@ -278,7 +278,7 @@
         term_w_fc2,
         term_b_fc2,
     ) = grads
-    wholes = lax.psum(
+    inner = lax.psum(
         (
             term_gain_one,
             term_shift_one,
@@ -294,8 +294,9 @@
             term_w_fc2,
             term_b_fc2,
         ),
-        ("replica", "group"),
-    )
+        "group",
+    )
+    wholes = lax.psum(inner, "replica")
     position = lax.axis_index("group")
     members = lax.axis_size("group")
     totals = tuple((owned_rows(whole, position, members) for whole in wholes))

time: 724 us -> 873 us (1.21)
  waiting for transfers between devices: 90.6 us -> 205 us
  blocking collectives: 71.9 us -> 109 us
    psum x1, waiting for transfers between devices: 89.2 us -> 153 us  [local(): lax.psum((term_gain_one, term_shift_one, term_w_qkv, term_b_query, term_b...]
    psum x0 -> x1, blocking collectives: none -> 61.7 us  [local(): wholes = lax.psum(inner, 'replica')]
    psum x0 -> x1, waiting for transfers between devices: none -> 50.8 us  [local(): wholes = lax.psum(inner, 'replica')]
    psum x1, blocking collectives: 39.7 us -> 7.41 us  [local(): lax.psum((term_gain_one, term_shift_one, term_w_qkv, term_b_query, term_b...]
    unnamed x100 -> x96, local copies, waits for them, and re-layouts: 49 us -> 50.7 us
  transfers between devices with their start and end apart: 3 -> 4, of which waited for: 1 -> 2; matrix products, arithmetic and copies ran while one was open for 40% -> 34% of each run, Pallas kernels for 0% -> 0%
where the time goes in v1:
time: 873 us; the launch traced here: 867 us
  matrix products  303 us (35%)
  waiting for transfers between devices  205 us (23%)
  local copies, waits for them, and re-layouts  176 us (20%)
  blocking collectives  109 us (12%)
  other arithmetic  59 us (7%)
  between operations  15.4 us (2%)
    psum x1, waiting for transfers between devices, local(): lax.psum((term_gain_one, term_shift_one, term_w_qkv, term_b_query, term_b...  153 us
    dot_general x4, matrix products, product(): return jnp.dot(left, right, preferred_element_type=jnp.float32)  86.9 us
    psum x1, blocking collectives, local(): wholes = lax.psum(inner, 'replica')  61.7 us
    psum x1, waiting for transfers between devices, local(): wholes = lax.psum(inner, 'replica')  50.8 us
    unnamed x96, local copies, waits for them, and re-layouts  50.7 us
    dot_general x4, matrix products, product_right_t(): lax.dot_general(left, right, (((1,), (1,)), ((), ())), preferred_element_...  48.8 us
    dot_general x1, matrix products, backward_pass(): jnp.einsum('bhst,bshe->bthe', grad_scores, query, preferred_element_type=...  41 us
    dot_general x1, matrix products, backward_pass(): jnp.einsum('bhst,bthe->bshe', grad_scores, keys, preferred_element_type=j...  36.2 us
  transfers between devices with their start and end apart: 4, of which 2 were waited for; matrix products, arithmetic and copies ran while one was open for 34% of the time, Pallas kernels for 0%

profile of v1, /device:TPU:0, one launch (start us, length us, event | category | flops | bytes accessed | tf_op | source)
XLA Modules:
  0.0 867.2 jit_solution(2639844314006322271)
XLA Ops:
  46.2 22.4 %all_gather.47 = bf16[384,1152]{1,0:T(8,128)(2,1)S(1)} all-gather(bf16[192,1152]{1,0:T(8,128)(2,1)S(1)} %copy-done.18), channel_id=1, replica_groups=mesh['replica'=16,'group'=2] {'group'}, dimensions={0}, use_global_device_ids=true | all-gather | bytes 1327104 | tf_op jit(solution)/shard_map/all_gather | solution.py:237
  72.1 8.7 %fusion.17 = bf16[3940,1152]{1,0:T(8,128)(2,1)} fusion(bf16[384,1152]{1,0:T(8,128)(2,1)S(1)} %all_gather.47, f32[1152]{0:T(1024)S(1)} %maximum_convert_fusion.1, f32[3940,384]{1,0:T(8,128)S(1)} %copy-done.1, f32[384]{0:T(512)S(1)} %copy-done.27, f32[384]{0:T(512)S(1)} %copy-done.25, f32[3940]{0:T(1024)S(1)} %copy-done.23, f32[3940]{0:T(1024)S(1)} %div.27), kind=kOutput, calls=%fused_computation.34 | convolution fusion | flops 3502502400 | bytes 16053536 | tf_op jit(solution)/shard_map/dot_general | solution.py:11
  80.7 27.6 %reshape.236 = bf16[20,197,3,6,64]{4,3,2,1,0:T(8,128)(2,1)} reshape(bf16[3940,1152]{1,0:T(8,128)(2,1)} %fusion.17) | data formatting | bytes 18155520 | tf_op jit(solution)/shard_map/reshape | solution.py:80
  108.4 16.3 %fusion.67 = (bf16[20,197,1,6,64]{4,3,2,1,0:T(8,128)(2,1)}, bf16[20,197,1,6,64]{4,3,2,1,0:T(8,128)(2,1)}, bf16[20,197,1,6,64]{4,3,2,1,0:T(8,128)(2,1)}) fusion(bf16[20,197,3,6,64]{4,3,2,1,0:T(8,128)(2,1)} %reshape.236), kind=kLoop, calls=%fused_computation.116 | loop fusion | bytes 18155520 | tf_op jit(solution)/shard_map/slice | solution.py:81
  124.7 9.7 %copy.74 = bf16[20,197,1,6,64]{1,4,3,0,2:T(8,128)(2,1)} copy(bf16[20,197,1,6,64]{4,3,2,1,0:T(8,128)(2,1)} %get-tuple-element.59) | data formatting | bytes 6051840
  134.4 9.7 %copy.75 = bf16[20,197,1,6,64]{1,4,3,0,2:T(8,128)(2,1)} copy(bf16[20,197,1,6,64]{4,3,2,1,0:T(8,128)(2,1)} %get-tuple-element.61) | data formatting | bytes 6051840
  144.1 14.9 %multiply_reduce_fusion.1 = (f32[20,6,197]{2,1,0:T(8,128)S(1)}, f32[20,6,197,197]{2,3,1,0:T(8,128)}) fusion(bf16[20,197,1,6,64]{1,4,3,0,2:T(8,128)(2,1)} %copy.75, bf16[20,197,1,6,64]{1,4,3,0,2:T(8,128)(2,1)} %copy.74), kind=kOutput, calls=%fused_computation.32 | convolution fusion | flops 605396736 | bytes 24774720 | tf_op jit(solution)/shard_map/bshe,bthe->bhst/dot_general | solution.py:53
  159.0 10.6 %exponential_reduce_fusion = f32[20,6,197]{2,1,0:T(8,128)S(1)} fusion(f32[20,6,197,197]{2,3,1,0:T(8,128)} %get-tuple-element.63, f32[20,6,197]{2,1,0:T(8,128)S(1)} %is-finite_select_fusion), kind=kLoop, calls=%fused_computation.7 | loop fusion | flops 13947600 | bytes 18817440 | tf_op jit(solution)/shard_map/reduce_sum | solution.py:85
  169.7 9.9 %copy.73 = bf16[20,197,1,6,64]{1,4,3,0,2:T(8,128)(2,1)} copy(bf16[20,197,1,6,64]{4,3,2,1,0:T(8,128)(2,1)} %get-tuple-element.60) | data formatting | bytes 6051840
  179.6 15.8 %convert_bitcast_fusion = bf16[20,197,6,64]{1,3,2,0:T(8,128)(2,1)} fusion(bf16[20,197,1,6,64]{1,4,3,0,2:T(8,128)(2,1)} %copy.73, f32[20,6,197]{2,1,0:T(8,128)S(1)} %log_add_fusion, f32[20,6,197,197]{2,3,1,0:T(8,128)} %get-tuple-element.63), kind=kOutput, calls=%fused_computation.73 | convolution fusion | flops 611590464 | bytes 24774720 | tf_op jit(solution)/shard_map/bhst,bthe->bshe/dot_general | solution.py:87
  195.4 6.8 copy.57
  235.9 62.0 %fusion.4 = (bf16[3940,1536]{1,0:T(8,128)(2,1)}, f32[3940,1536]{1,0:T(8,128)}) fusion(f32[1536]{0:T(1024)S(1)} %reshape.219, bf16[384,1536]{1,0:T(8,128)(2,1)} %all-gather.4.cloned.1.call-done, f32[3940,384]{1,0:T(8,128)} %copy-done.2, f32[384]{0:T(512)S(1)} %convert_element_type.115, f32[384]{0:T(512)S(1)} %convert_element_type.114, ...), kind=kOutput, calls=%fused_computation.10 | convolution fusion | flops 5054799360 | bytes 43583264 | tf_op jit(solution)/shard_map/dot_general | solution.py:11
  297.9 20.8 %fusion.71 = (f32[1536]{0:T(1024)}, bf16[3940,1536]{1,0:T(8,128)(2,1)}) fusion(f32[3940,1536]{1,0:T(8,128)} %get-tuple-element.67, f32[1536]{0:T(1024)S(1)} %reshape.219, bf16[3940,384]{1,0:T(8,128)(2,1)S(1)} %copy-done.9, bf16[1536,384]{1,0:T(8,128)(2,1)} %all-gather.6.cloned.1.call-done), kind=kOutput, calls=%fused_computation.118 | convolution fusion | flops 4720433664 | bytes 40528896 | tf_op jit(solution)/shard_map/dot_general | solution.py:21
  318.7 11.3 %fusion.27 = f32[384,1536]{1,0:T(8,128)} fusion(bf16[3940,1536]{1,0:T(8,128)(2,1)} %get-tuple-element.75, f32[3940,384]{1,0:T(8,128)S(1)} %copy-done.3, f32[384]{0:T(512)S(1)} %convert_element_type.115, f32[384]{0:T(512)S(1)} %convert_element_type.114, f32[3940]{0:T(1024)S(1)} %add_rsqrt_fusion.1, f32[3940]{0:T(1024)S(1)} %broadcast_multiply_fusion.5), kind=kOutput, calls=%fused_computation.49 | convolution fusion | flops 4655377920 | bytes 20549408 | tf_op jit(solution)/shard_map/dot_general | solution.py:15
  330.0 11.0 %multiply_reduce_fusion.3 = (f32[384]{0:T(512)S(1)}, f32[3940]{0:T(1024)S(1)}, f32[3940]{0:T(1024)S(1)}, f32[384]{0:T(512)S(1)}, f32[3940,384]{1,0:T(8,128)S(1)}) fusion(f32[3940,384]{1,0:T(8,128)S(1)} %copy-done.3, f32[3940]{0:T(1024)S(1)} %add_rsqrt_fusion.1, f32[3940]{0:T(1024)S(1)} %broadcast_multiply_fusion.5, f32[384]{0:T(512)S(1)} %convert_element_type.114, ...), kind=kOutput, calls=%fused_computation.43 | convolution fusion | flops 4661420544 | bytes 25454656 | tf_op jit(solution)/shard_map/dot_general | solution.py:21
  349.7 7.4 reshape.237
  357.0 9.9 %copy.59 = bf16[20,197,6,64]{1,3,2,0:T(8,128)(2,1)} copy(bf16[20,197,6,64]{3,2,1,0:T(8,128)(2,1)} %reshape.237) | data formatting | bytes 6051840 | tf_op jit(solution)/shard_map/reshape | solution.py:164
  367.0 14.9 %fusion.36 = f32[20,6,197,197]{2,3,1,0:T(8,128)} fusion(bf16[20,197,6,64]{1,3,2,0:T(8,128)(2,1)} %copy.59, bf16[20,197,1,6,64]{1,4,3,0,2:T(8,128)(2,1)} %copy.73), kind=kOutput, calls=%fused_computation.69 | convolution fusion | flops 596106240 | bytes 24680160 | tf_op jit(solution)/shard_map/bshe,bthe->bhst/dot_general | solution.py:170
  381.9 36.2 %bitcast_reduce_fusion.1 = (f32[6,64]{1,0:T(8,128)S(1)}, bf16[20,6,64,197]{3,2,1,0:T(8,128)(2,1)}) fusion(f32[20,6,197,197]{2,3,1,0:T(8,128)} %fusion.36, f32[20,6,197]{2,1,0:T(8,128)S(1)} %copy-done.16, f32[20,6,197,197]{2,3,1,0:T(8,128)} %get-tuple-element.63, bf16[20,197,1,6,64]{1,4,3,0,2:T(8,128)(2,1)} %copy.75), kind=kOutput, calls=%fused_computation.39 | convolution fusion | flops 641069312 | bytes 43404576 | tf_op jit(solution)/shard_map/bhst,bthe->bshe/dot_general | solution.py:175
  418.1 41.0 %fusion.40 = bf16[20,197,1,6,64]{1,4,3,0,2:T(8,128)(2,1)} fusion(f32[20,6,197,197]{2,3,1,0:T(8,128)} %fusion.36, f32[20,6,197]{2,1,0:T(8,128)S(1)} %copy-done.16, f32[20,6,197,197]{2,3,1,0:T(8,128)} %get-tuple-element.63, bf16[20,197,1,6,64]{1,4,3,0,2:T(8,128)(2,1)} %copy.74), kind=kOutput, calls=%fused_computation.74 | convolution fusion | flops 638043776 | bytes 43403040 | tf_op jit(solution)/shard_map/bhst,bshe->bthe/dot_general | solution.py:178
  459.2 13.8 %bitcast_reduce_fusion = (f32[6,64]{1,0:T(8,128)S(1)}, bf16[20,6,64,197]{3,2,1,0:T(8,128)(2,1)}) fusion(bf16[20,197,6,64]{1,3,2,0:T(8,128)(2,1)} %copy.59, f32[20,6,197]{2,1,0:T(8,128)S(1)} %copy-done.16, f32[20,6,197,197]{2,3,1,0:T(8,128)} %get-tuple-element.63), kind=kOutput, calls=%fused_computation.38 | convolution fusion | flops 613103040 | bytes 24776256 | tf_op jit(solution)/shard_map/bhst,bshe->bthe/dot_general | solution.py:167
  473.0 6.9 maximum_convert_fusion
  479.9 9.9 %copy.64 = bf16[20,197,3,6,64]{1,0,4,3,2:T(8,128)(2,1)} copy(bf16[20,197,3,6,64]{1,4,3,0,2:T(8,128)(2,1)S(1)} %maximum_convert_fusion) | data formatting | bytes 18155520 | tf_op jit(solution)/shard_map/convert_element_type | solution.py:186
  489.8 20.9 %convert_element_type.127 = bf16[3940,1152]{0,1:T(8,128)(2,1)} reshape(bf16[20,197,3,6,64]{1,0,4,3,2:T(8,128)(2,1)} %copy.64) | data formatting | bytes 18155520 | tf_op jit(solution)/shard_map/convert_element_type | solution.py:186
  510.6 10.8 %fusion.73 = f32[1536,384]{1,0:T(8,128)} fusion(bf16[3940,1536]{1,0:T(8,128)(2,1)} %get-tuple-element.66, bf16[3940,384]{1,0:T(8,128)(2,1)S(1)} %copy-done.10), kind=kOutput, calls=%fused_computation.120 | convolution fusion | flops 4647813120 | bytes 17488896 | tf_op jit(solution)/shard_map/dot_general | solution.py:15
  529.5 14.7 %multiply_reduce_fusion.4 = (f32[384]{0:T(512)S(1)}, f32[3940]{0:T(1024)S(1)}, f32[3940]{0:T(1024)S(1)}, f32[384]{0:T(512)S(1)}, f32[3940,384]{1,0:T(8,128)}) fusion(f32[3940,384]{1,0:T(8,128)} %reshape.192, f32[3940]{0:T(1024)S(1)} %copy-done.24, f32[3940]{0:T(1024)S(1)} %copy-done.22, f32[384]{0:T(512)S(1)} %copy-done.26, ...), kind=kOutput, calls=%fused_computation.44 | convolution fusion | flops 3499467776 | bytes 22133824 | tf_op jit(solution)/shard_map/dot_general | solution.py:21
  544.2 153.3 %all-reduce.18.cloned.1.call-done = (f32[384,1152]{1,0:T(8,128)}, f32[384,384]{1,0:T(8,128)}, f32[384,1536]{1,0:T(8,128)}, f32[1536,384]{1,0:T(8,128)}) async-done(((f32[384,1152]{1,0:T(8,128)}, f32[384,384]{1,0:T(8,128)}, f32[384,1536]{1,0:T(8,128)}, f32[1536,384]{1,0:T(8,128)}), (f32[384,1152]{1,0:T(8,128)}, f32[384,384]{1,0:T(8,128)}, f32[384,1536]{1,0:T(8,128)}, ...) | async-done | bytes 7077904 | tf_op jit(solution)/shard_map/psum | solution.py:281
  697.5 10.4 %multiply_add_fusion = f32[3940,384]{1,0:T(8,128)} fusion(f32[3940,384]{1,0:T(8,128)} %copy-done, f32[3940,384]{1,0:T(8,128)} %get-tuple-element.69, f32[3940,384]{1,0:T(8,128)} %reshape.192, f32[3940]{0:T(1024)S(1)} %broadcast_multiply_fusion.1, f32[3940]{0:T(1024)S(1)} %broadcast_multiply_fusion.2, f32[384]{0:T(512)S(1)} %copy-done.26, ...), kind=kLoop, calls=%fused_computation.45 | loop fusion | flops 12103680 | bytes 24271936 | tf_op jit(solution)/shard_map/add | solution.py:193
  713.5 10.8 %add_convert_fusion.1 = bf16[3940,384]{1,0:T(8,128)(2,1)S(1)} fusion(f32[3940,384]{1,0:T(8,128)} %copy-done.2, bf16[3940,1536]{1,0:T(8,128)(2,1)} %get-tuple-element.66, bf16[1536,384]{1,0:T(8,128)(2,1)} %all-gather.6.cloned.1.call-done, f32[384]{0:T(512)S(1)} %convert_element_type.119), kind=kOutput, calls=%fused_computation.53 | convolution fusion | flops 4652352000 | bytes 22362624 | tf_op jit(solution)/shard_map/dot_general | solution.py:11
  726.8 7.4 all-reduce.10
  734.2 61.7 %all-reduce.8 = (f32[384]{0:T(512)S(1)}, f32[384]{0:T(512)S(1)}, f32[384]{0:T(512)S(1)}, f32[384]{0:T(512)S(1)}, f32[384]{0:T(512)S(1)}, /*index=5*/f32[384]{0:T...) all-reduce(f32[384]{0:T(512)S(1)} %get-tuple-element.36, ...), channel_id=1, replica_groups=mesh['replica'=16,'group'=2] {'replica'}, use_global_device_ids=true, to_apply=%region_13.0 | all-reduce | flops 4608 | bytes 36864 | tf_op jit(solution)/shard_map/psum | solution.py:299
  801.7 50.8 %all-reduce.16.cloned.1.call-done = (f32[384,1152]{1,0:T(8,128)}, f32[384,384]{1,0:T(8,128)}, f32[384,1536]{1,0:T(8,128)}, f32[1536,384]{1,0:T(8,128)}) async-done(((f32[384,1152]{1,0:T(8,128)}, f32[384,384]{1,0:T(8,128)}, f32[384,1536]{1,0:T(8,128)}, f32[1536,384]{1,0:T(8,128)}), (f32[384,1152]{1,0:T(8,128)}, f32[384,384]{1,0:T(8,128)}, f32[384,1536]{1,0:T(8,128)}, ...) | async-done | bytes 7077904 | tf_op jit(solution)/shard_map/psum | solution.py:299
  (157 shorter events, 113.4 us)
Async XLA Ops:
  7.2 4.2 copy-start.4
  7.2 228.7 %all-gather.4.cloned.1.call-start = ((), (), s32[]{:S(2)}) async-start(), calls=%async_computation | async-start | bytes 1769472 | tf_op jit(solution)/shard_map/all_gather | solution.py:244
  7.9 290.0 %all-gather.6.cloned.1.call-start = ((), (), s32[]{:S(2)}) async-start(), calls=%async_computation.1 | async-start | bytes 1769472 | tf_op jit(solution)/shard_map/all_gather | solution.py:246
  8.7 688.8 %all-reduce.18.cloned.1.call-start = ((), (), s32[]{:S(2)}) async-start(), calls=%async_computation.3 | async-start | bytes 14155776 | tf_op jit(solution)/shard_map/psum | solution.py:281
  11.4 34.8 %copy-start.18 = (bf16[192,1152]{1,0:T(8,128)(2,1)S(1)}, bf16[192,1152]{1,0:T(8,128)(2,1)}, u32[]{:S(2)}) copy-start(bf16[192,1152]{1,0:T(8,128)(2,1)} %param.19) | copy-start | bytes 1327108
  13.7 58.3 %copy-start.21 = (f32[3940]{0:T(1024)}, f32[3940]{0:T(1024)S(1)}, u32[]{:S(2)}) copy-start(f32[3940]{0:T(1024)S(1)} %div.27) | copy-start | bytes 47284
  46.2 25.8 %copy-start.34 = (bf16[384]{0:T(512)(128)(2,1)S(1)}, bf16[384]{0:T(512)(128)(2,1)}, u32[]{:S(2)}) copy-start(bf16[384]{0:T(512)(128)(2,1)} %get-tuple-element.49) | copy-start | bytes 2308
  46.2 25.8 %copy-start.35 = (bf16[384]{0:T(512)(128)(2,1)S(1)}, bf16[384]{0:T(512)(128)(2,1)}, u32[]{:S(2)}) copy-start(bf16[384]{0:T(512)(128)(2,1)} %get-tuple-element.50) | copy-start | bytes 2308
  46.2 25.8 %copy-start.1 = (f32[3940,384]{1,0:T(8,128)S(1)}, f32[3940,384]{1,0:T(8,128)}, u32[]{:S(2)}) copy-start(f32[3940,384]{1,0:T(8,128)} %reshape.192) | copy-start | bytes 18155524
  46.2 25.8 %copy-start.23 = (f32[3940]{0:T(1024)S(1)}, f32[3940]{0:T(1024)}, u32[]{:S(2)}) copy-start(f32[3940]{0:T(1024)} %rsqrt.21) | copy-start | bytes 47284
  46.2 25.8 %copy-start.25 = (f32[384]{0:T(512)S(1)}, f32[384]{0:T(512)}, u32[]{:S(2)}) copy-start(f32[384]{0:T(512)} %convert_element_type.105) | copy-start | bytes 4612
  46.2 25.8 %copy-start.27 = (f32[384]{0:T(512)S(1)}, f32[384]{0:T(512)}, u32[]{:S(2)}) copy-start(f32[384]{0:T(512)} %convert_element_type.106) | copy-start | bytes 4612
  169.6 25.8 %copy-start.15 = (f32[20,6,197]{2,1,0:T(8,128)}, f32[20,6,197]{2,1,0:T(8,128)S(1)}, u32[]{:S(2)}) copy-start(f32[20,6,197]{2,1,0:T(8,128)S(1)} %log_add_fusion) | copy-start | bytes 283684
  195.4 13.4 %copy-start.33 = (bf16[384]{0:T(512)(128)(2,1)S(1)}, bf16[384]{0:T(512)(128)(2,1)}, u32[]{:S(2)}) copy-start(bf16[384]{0:T(512)(128)(2,1)} %get-tuple-element.53) | copy-start | bytes 2308
  195.4 13.4 %copy-start.19 = (bf16[192,384]{1,0:T(8,128)(2,1)S(1)}, bf16[192,384]{1,0:T(8,128)(2,1)}, u32[]{:S(2)}) copy-start(bf16[192,384]{1,0:T(8,128)(2,1)} %param.22) | copy-start | bytes 442372
  208.8 11.2 %copy-start.5 = (bf16[3940,384]{0,1:T(8,128)(2,1)}, bf16[3940,384]{0,1:T(8,128)(2,1)S(1)}, u32[]{:S(2)}) copy-start(bf16[3940,384]{0,1:T(8,128)(2,1)S(1)} %reshape.187) | copy-start | bytes 9077764
  214.7 5.4 copy-start.13
  220.1 4.4 copy-start.32
  220.1 4.4 copy-start.31
  220.1 4.4 copy-start.29
  220.1 9.1 %copy-start.7 = (bf16[20,197,384]{2,1,0:T(8,128)(2,1)S(1)}, bf16[20,197,384]{2,1,0:T(8,128)(2,1)}, u32[]{:S(2)}) copy-start(bf16[20,197,384]{2,1,0:T(8,128)(2,1)} %param.16) | copy-start | bytes 9077764
  235.9 62.1 %copy-start.9 = (bf16[3940,384]{1,0:T(8,128)(2,1)S(1)}, bf16[3940,384]{1,0:T(8,128)(2,1)}, u32[]{:S(2)}) copy-start(bf16[3940,384]{1,0:T(8,128)(2,1)} %reshape.189) | copy-start | bytes 9077764
  297.9 20.8 %copy-start.3 = (f32[3940,384]{1,0:T(8,128)S(1)}, f32[3940,384]{1,0:T(8,128)}, u32[]{:S(2)}) copy-start(f32[3940,384]{1,0:T(8,128)} %copy-done.2) | copy-start | bytes 18155524
  318.7 11.3 %copy-start.36 = (bf16[384,1536]{1,0:T(8,128)(2,1)S(1)}, bf16[384,1536]{1,0:T(8,128)(2,1)}, u32[]{:S(2)}) copy-start(bf16[384,1536]{1,0:T(8,128)(2,1)} %all-gather.4.cloned.1.call-done) | copy-start | bytes 3538948
  341.0 3.5 copy-start.6
  367.0 14.9 %copy-start.16 = (f32[20,6,197]{2,1,0:T(8,128)S(1)}, f32[20,6,197]{2,1,0:T(8,128)}, u32[]{:S(2)}) copy-start(f32[20,6,197]{2,1,0:T(8,128)} %copy-done.15) | copy-start | bytes 283684
  489.8 20.9 %copy-start.10 = (bf16[3940,384]{1,0:T(8,128)(2,1)S(1)}, bf16[3940,384]{1,0:T(8,128)(2,1)}, u32[]{:S(2)}) copy-start(bf16[3940,384]{1,0:T(8,128)(2,1)} %reshape.189) | copy-start | bytes 9077764
  510.6 10.8 %copy-start.11 = (bf16[3940,1152]{0,1:T(8,128)(2,1)S(1)}, bf16[3940,1152]{0,1:T(8,128)(2,1)}, u32[]{:S(2)}) copy-start(bf16[3940,1152]{0,1:T(8,128)(2,1)} %convert_element_type.127) | copy-start | bytes 27233284
  510.6 10.8 %copy-start.12 = (bf16[3940,384]{1,0:T(8,128)(2,1)S(1)}, bf16[3940,384]{1,0:T(8,128)(2,1)}, u32[]{:S(2)}) copy-start(bf16[3940,384]{1,0:T(8,128)(2,1)} %convert_element_type.129) | copy-start | bytes 9077764
  527.1 325.4 %all-reduce.16.cloned.1.call-start = ((), (), s32[]{:S(2)}) async-start(), calls=%async_computation.2 | async-start | bytes 14155776 | tf_op jit(solution)/shard_map/psum | solution.py:299
  713.5 13.3 %copy-start.28 = (f32[1536]{0:T(1024)S(1)}, f32[1536]{0:T(1024)}, u32[]{:S(2)}) copy-start(f32[1536]{0:T(1024)} %get-tuple-element.74) | copy-start | bytes 18436
  852.5 7.0 copy-start.20
  (9 other events, 22.0 us)
Sparse Core Ops, SparseCore 0:
  9.5 25.4 all-gather.3
  36.6 31.9 all-gather.5
  527.2 170.2 all-reduce.17
  701.4 151.0 all-reduce.15
